TPU v7x, 512 devices: a whole 4x4x16 slice. The times are simulated.
512 devices in a mesh: grp: 16 (over z), cand: 32 (over y, x, core).
Axes of the slice: x: 4, y: 4, z: 16, core: 2. Of those that a mesh axis runs over, the one named last changes fastest.
Arguments:
- embeddings: bfloat16 [384, 1024, 1024], P('grp', 'cand'), may hold values from -6 to 6
- hidden_weight: bfloat16 [2048, 1024], P('cand'), may hold values from -0.1875 to 0.1875
- score_weight: bfloat16 [2048], replicated, may hold values from -0.5 to 0.5
- relevance: int32 [384, 1024], P('grp', 'cand'), may hold values from 0 to 4
- rank_pos: int32 [384, 1024], P('grp', 'cand'), may hold values from 0 to 1023, as said below
- ideal_dcg: float32 [384], P('grp'), may hold values from 32 to 128
Outputs:
- grad_hidden: float32 [2048, 1024], P('cand')
- lambdas: float32 [384, 1024], P('grp', 'cand')
Inputs may be any that keep to these rules, and one draw needn't show every extreme that they name: `rank_pos`: in each group the rank positions are a permutation of 0 to 1023.
All inputs are finite; a program needn't handle non-finite values.
Results may differ from a plain program's by a relative error of at most 0.006.
Values may be sent and summed in bfloat16 or wider, within the bound.
No kernel may reach another device: no remote copies, remote signals or barrier semaphores. Data moves between devices by JAX's collectives and lax.ppermute only.
A program may use at most 64 MiB of HBM per device.

v0:
```python
import jax
import jax.numpy as jnp
from jax import lax
from jax.sharding import PartitionSpec as P

EPS = 1e-06


def turned_gather(arrays, axis, dims):
    turned = [jnp.moveaxis(a, dim, 0) for a, dim in zip(arrays, dims)]
    widths = [t[0].size for t in turned]
    both = jnp.concatenate([t.reshape(-1, w) for t, w in zip(turned, widths)], axis=1)
    result = lax.all_gather(both, axis, axis=0, tiled=True)
    parts = jnp.split(result, [sum(widths[:k]) for k in range(1, len(widths))], axis=1)
    return tuple(
        (
            jnp.moveaxis(b.reshape(-1, *t.shape[1:]), 0, dim)
            for b, t, dim in zip(parts, turned, dims)
        )
    )


def copy_for_each(value, axis):
    copies = jnp.broadcast_to(value, (lax.axis_size(axis), *value.shape))
    return lax.all_to_all(copies, axis, split_axis=0, concat_axis=0, tiled=True)


def joined_along(parts, dim):
    parts = jnp.moveaxis(parts, 0, dim)
    shape = parts.shape
    return parts.reshape(*shape[:dim], shape[dim] * shape[dim + 1], *shape[dim + 2 :])


def gathered_copies(value, axis, dim):
    parts = copy_for_each(value, axis)
    return joined_along(parts, dim)


def over_copies(value, axis):
    return copy_for_each(value, axis).sum(axis=0)


def pair_lambdas(own_score, own_gain, own_disc, far_score, far_gain, far_disc, ideal):
    gain_diff = far_gain[..., None, :] - own_gain[..., :, None]
    toward = jnp.sign(gain_diff)
    weight = (
        jnp.abs(gain_diff)
        * jnp.abs(far_disc[..., None, :] - own_disc[..., :, None])
        / ideal[..., None, None]
    )
    margin = own_score[..., :, None] - far_score[..., None, :]
    return jnp.sum(weight * toward * jax.nn.sigmoid(toward * margin), axis=-1)


def gain_of(labels):
    return jnp.exp2(labels.astype(jnp.float32)) - 1.0


def discount_of(positions):
    return 1.0 / jnp.log2(2.0 + positions.astype(jnp.float32))


def per_device(embeddings, hidden_weight, score_weight, relevance, rank_pos, ideal_dcg):
    grp_count, local, width = embeddings.shape
    cand_rows = embeddings.reshape(grp_count * local, width)
    all_labels, all_ranks = turned_gather((relevance, rank_pos), "cand", (1, 1))
    all_gain = gain_of(all_labels)
    all_disc = discount_of(all_ranks)
    pre_act = lax.dot_general(
        cand_rows,
        lax.all_gather(hidden_weight, "cand", axis=0, tiled=True),
        (((1,), (1,)), ((), ())),
        preferred_element_type=jnp.float32,
    )
    acts, pull = jax.vjp(jax.nn.gelu, pre_act)
    scores = jnp.dot(
        acts.astype(jnp.bfloat16), score_weight, preferred_element_type=jnp.float32
    ).reshape(grp_count, local)
    gain_vals = gain_of(relevance)
    discount = discount_of(rank_pos)
    lambdas = pair_lambdas(
        scores,
        gain_vals,
        discount,
        gathered_copies(scores, "cand", 1),
        all_gain,
        all_disc,
        ideal_dcg,
    )
    upstream = (
        lambdas.reshape(grp_count * local)[:, None] * score_weight.astype(jnp.float32)[None, :]
    )
    grad_pre = pull(upstream)[0].astype(jnp.bfloat16)
    owned = lax.psum_scatter(
        lax.dot_general(
            grad_pre, cand_rows, (((0,), (0,)), ((), ())), preferred_element_type=jnp.float32
        ).astype(jnp.bfloat16),
        "cand",
        scatter_dimension=0,
        tiled=True,
    ).astype(jnp.float32)
    summed = lax.psum(owned, "grp")
    squares = over_copies(jnp.sum(summed * summed), "cand")
    entries = summed.shape[0] * summed.shape[1] * lax.axis_size("cand")
    scale = lax.rsqrt(squares / entries + EPS)
    return (summed * scale, lambdas)


def solution(mesh):
    return jax.shard_map(
        per_device,
        mesh=mesh,
        in_specs=(
            P("grp", "cand", None),
            P("cand", None),
            P(),
            P("grp", "cand"),
            P("grp", "cand"),
            P("grp"),
        ),
        out_specs=(P("cand", None), P("grp", "cand")),
        check_vma=False,
    )
```

profile of v0, /device:TPU:1, one launch (start us, length us, event | category | flops | bytes accessed | tf_op | source)
XLA Modules:
  0.0 302.9 jit_solution(5547443069772350048)
XLA Ops:
  7.2 0.0 copy-start
  7.2 0.0 all-gather.2.cloned.1.call-start
  7.2 0.7 all-gather.2.cloned.1.call-update
  7.9 0.7 reshape.20
  8.6 0.8 copy.28
  9.4 0.8 copy.29
  10.2 0.1 pad_add_fusion
  10.2 28.5 %all_gather.6 = s32[1024,48]{1,0:T(8,128)S(1)} all-gather(s32[32,48]{1,0:T(8,128)S(1)} %pad_add_fusion), channel_id=1, replica_groups=mesh['grp'=16,'cand'=32] {'cand'}, dimensions={0}, use_global_device_ids=true | all-gather | bytes 202752 | tf_op jit(solution)/shard_map/all_gather | solution.py:13
  38.7 0.2 fusion.33
  38.9 0.2 copy.35
  39.1 0.2 copy.36
  39.3 0.1 divide_bitcast_fusion
  39.3 38.9 %all-gather.2.cloned.1.call-done = bf16[2048,1024]{1,0:T(8,128)(2,1)} async-done(((bf16[64,1024]{1,0:T(8,128)(2,1)}), bf16[2048,1024]{1,0:T(8,128)(2,1)}) %all-gather.2.cloned.1.call-update) | async-done | bytes 4194320 | tf_op jit(solution)/shard_map/all_gather | solution.py:71
  78.2 0.0 copy-done
  78.2 5.3 %fusion.34 = f32[768,2048]{1,0:T(8,128)S(1)} fusion(bf16[768,1024]{1,0:T(8,128)(2,1)S(1)} %bitcast.12, bf16[2048,1024]{1,0:T(8,128)(2,1)} %all-gather.2.cloned.1.call-done), kind=kOutput, calls=%fused_computation.48 | convolution fusion | flops 3221225472 | bytes 12058624 | tf_op jit(solution)/shard_map/dot_general | solution.py:69
  83.5 0.0 copy-start.6
  83.5 2.7 copy-done.6
  86.1 0.0 copy-start.1
  86.1 0.0 copy-start.2
  86.1 0.0 copy-start.3
  86.1 0.0 copy-start.5
  86.1 2.2 fusion.22
  88.4 0.1 sub.63
  88.5 0.8 reshape.24
  89.3 5.3 %all-to-all-start = ((f32[32,1,768]{2,1,0:T(1,128)}), f32[32,1,768]{2,1,0:T(1,128)S(1)}, u32[]{:S(2)}, u32[]{:S(2)}) async-start(f32[32,1,768]{2,1,0:T(1,128)} %reshape.24), calls=%async_computation | async-start | bytes 196608 | tf_op jit(solution)/shard_map/all_to_all | solution.py:25
  94.6 0.0 reduce-scatter.2.cloned.1.call-start
  94.7 0.0 copy-done.1
  94.7 0.0 copy-done.2
  94.7 0.0 copy-done.3
  94.7 7.3 %all-to-all-done = f32[32,1,768]{2,1,0:T(1,128)S(1)} async-done(((f32[32,1,768]{2,1,0:T(1,128)}), f32[32,1,768]{2,1,0:T(1,128)S(1)}, u32[]{:S(2)}, u32[]{:S(2)}) %all-to-all-start) | async-done | bytes 98336 | tf_op jit(solution)/shard_map/all_to_all | solution.py:25
  102.0 0.5 broadcast.84
  102.5 0.9 reduce.3
  103.4 0.1 reshape.25
  103.6 0.1 copy.32
  103.6 0.2 sub.65
  103.8 0.0 copy-done.5
  103.8 3.0 fusion.13
  106.8 0.0 copy-start.4
  106.8 0.1 mul.88
  106.9 10.4 %convolution_convert_fusion = bf16[2048,1024]{1,0:T(8,128)(2,1)} fusion(bf16[768,1024]{1,0:T(8,128)(2,1)S(1)} %bitcast.13, f32[768,2048]{1,0:T(8,128)} %copy-done.6, f32[2048]{0:T(1024)S(1)} %convert_element_type.34, f32[768]{0:T(1024)S(1)} %mul.88), kind=kOutput, calls=%fused_computation.19 | convolution fusion | flops 3256352768 | bytes 12069888 | tf_op jit(solution)/shard_map/dot_general | solution.py:95
  117.3 0.0 copy-done.4
  117.3 0.0 reduce-scatter.2.cloned.1.call-update
  117.3 101.5 %reduce-scatter.2.cloned.1.call-done = bf16[64,1024]{1,0:T(8,128)(2,1)} async-done(((bf16[2048,1024]{1,0:T(8,128)(2,1)}), bf16[64,1024]{1,0:T(8,128)(2,1)}) %reduce-scatter.2.cloned.1.call-update) | async-done | bytes 131088 | tf_op jit(solution)/shard_map/reduce_scatter | solution.py:94
  218.8 46.8 %all-reduce.1 = f32[64,1024]{1,0:T(8,128)S(1)} all-reduce(bf16[64,1024]{1,0:T(8,128)(2,1)} %reduce-scatter.2.cloned.1.call-done), channel_id=1, replica_groups=mesh['grp'=16,'cand'=32] {'grp'}, use_global_device_ids=true, to_apply=%region_2.0 | all-reduce | flops 65536 | bytes 393216 | tf_op jit(solution)/shard_map/psum | solution.py:102
  265.6 0.7 multiply_reduce_fusion
  266.2 0.7 broadcast_in_dim.5
  266.9 27.1 %all_to_all.11 = f32[32,1,1]{2,1,0:T(1,128)S(1)} all-to-all(f32[32,1,1]{2,1,0:T(1,128)S(1)} %broadcast_in_dim.5), channel_id=1, replica_groups=mesh['grp'=16,'cand'=32] {'cand'}, dimensions={0} | all-to-all | bytes 256 | tf_op jit(solution)/shard_map/all_to_all | solution.py:25
  294.0 0.6 reduce_sum.29
  295.4 0.7 broadcast_multiply_fusion
  (3 shorter events, 0.1 us)
Async XLA Ops:
  7.2 71.0 %copy-start = (bf16[24,32,1024]{2,1,0:T(8,128)(2,1)S(1)}, bf16[24,32,1024]{2,1,0:T(8,128)(2,1)}, u32[]{:S(2)}) copy-start(bf16[24,32,1024]{2,1,0:T(8,128)(2,1)} %param.6) | copy-start | bytes 4718596
  7.2 71.0 %all-gather.2.cloned.1.call-start = ((), (), s32[]{:S(2)}) async-start(), calls=%async_computation.3 | async-start | bytes 4325376 | tf_op jit(solution)/shard_map/all_gather | solution.py:71
  83.5 2.7 copy-start.6
  86.1 8.6 %copy-start.1 = (s32[24,32]{1,0:T(8,128)S(1)}, s32[24,32]{1,0:T(8,128)}, u32[]{:S(2)}) copy-start(s32[24,32]{1,0:T(8,128)} %param.10) | copy-start | bytes 9220
  86.1 8.6 %copy-start.2 = (s32[24,32]{1,0:T(8,128)S(1)}, s32[24,32]{1,0:T(8,128)}, u32[]{:S(2)}) copy-start(s32[24,32]{1,0:T(8,128)} %param.9) | copy-start | bytes 9220
  86.1 8.6 %copy-start.3 = (bf16[2048]{0:T(1024)(128)(2,1)S(1)}, bf16[2048]{0:T(1024)(128)(2,1)}, u32[]{:S(2)}) copy-start(bf16[2048]{0:T(1024)(128)(2,1)} %param.8) | copy-start | bytes 12292
  86.1 17.7 %copy-start.5 = (f32[24]{0:T(128)S(1)}, f32[24]{0:T(128)}, u32[]{:S(2)}) copy-start(f32[24]{0:T(128)} %param.11) | copy-start | bytes 292
  89.3 12.7 %all-to-all-start = ((f32[32,1,768]{2,1,0:T(1,128)}), f32[32,1,768]{2,1,0:T(1,128)S(1)}, u32[]{:S(2)}, u32[]{:S(2)}) async-start(f32[32,1,768]{2,1,0:T(1,128)} %reshape.24), calls=%async_computation | async-start | bytes 196608 | tf_op jit(solution)/shard_map/all_to_all | solution.py:25
  94.6 124.2 %reduce-scatter.2.cloned.1.call-start = ((), (), s32[]{:S(2)}) async-start(), calls=%async_computation.4 | async-start | bytes 4325376 | tf_op jit(solution)/shard_map/reduce_scatter | solution.py:94
  106.8 10.5 %copy-start.4 = (f32[24,32]{1,0:T(8,128)}, f32[24,32]{1,0:T(8,128)S(1)}, u32[]{:S(2)}) copy-start(f32[24,32]{1,0:T(8,128)S(1)} %fusion.13) | copy-start | bytes 9220
Sparse Core Ops, SparseCore 0:
  11.1 67.0 all-gather.1
  117.5 101.2 reduce-scatter.1
where the time goes:
time: 303 us
  waiting for transfers between devices  148 us (49%)
  blocking collectives  102 us (34%)
  matrix products  17.9 us (6%)
  between operations  14.9 us (5%)
  local copies, waits for them, and re-layouts  8.06 us (3%)
  other arithmetic  6.06 us (2%)
  starting transfers between devices  5.38 us (2%)
    reduce_scatter x1, waiting for transfers between devices, per_device(): lax.psum_scatter(lax.dot_general(grad_pre, cand_rows, (((0,), (0,)), ((),...  101 us
    psum x1, blocking collectives, per_device(): summed = lax.psum(owned, 'grp')  46.8 us
    all_gather x1, waiting for transfers between devices, per_device(): lax.all_gather(hidden_weight, 'cand', axis=0, tiled=True)  38.9 us
    all_gather x1, blocking collectives, turned_gather(): result = lax.all_gather(both, axis, axis=0, tiled=True)  28.5 us
    all_to_all x1, blocking collectives, copy_for_each(): return lax.all_to_all(copies, axis, split_axis=0, concat_axis=0, tiled=True)  27.1 us
    dot_general x1, matrix products, per_device(): lax.dot_general(grad_pre, cand_rows, (((0,), (0,)), ((), ())), preferred_...  10.4 us
    all_to_all x1, waiting for transfers between devices, copy_for_each(): return lax.all_to_all(copies, axis, split_axis=0, concat_axis=0, tiled=True)  7.27 us
    unnamed x21, local copies, waits for them, and re-layouts  6.27 us
  transfers between devices with their start and end apart: 3, of which 3 were waited for; matrix products, arithmetic and copies ran while one was open for 1% of the time, Pallas kernels for 0%

commit v1 on v0

--- a/solution.py
+++ b/solution.py
@@ -99,7 +99,9 @@
         scatter_dimension=0,
         tiled=True,
     ).astype(jnp.float32)
-    summed = lax.psum(owned, "grp")
+    summed = owned
+    for hop in (1, 2, 4, 8):
+        summed = summed + lax.ppermute(summed, "grp", [(dev, dev ^ hop) for dev in range(16)])
     squares = over_copies(jnp.sum(summed * summed), "cand")
     entries = summed.shape[0] * summed.shape[1] * lax.axis_size("cand")
     scale = lax.rsqrt(squares / entries + EPS)

time: 303 us -> 327 us (1.079)
  blocking collectives: 102 us -> 40.5 us
  waiting for transfers between devices: 148 us -> 201 us
  starting transfers between devices: 5.38 us -> 36.6 us
    ppermute x0 -> x4, waiting for transfers between devices: none -> 52.2 us  [per_device(): lax.ppermute(summed, 'grp', [(dev, dev ^ hop) for dev in range(16)])]
    psum x1 -> x0, blocking collectives: 46.8 us -> none  [per_device(): summed = lax.psum(owned, 'grp')]
    ppermute x0 -> x4, starting transfers between devices: none -> 31.2 us  [per_device(): lax.ppermute(summed, 'grp', [(dev, dev ^ hop) for dev in range(16)])]
    all_to_all x1, blocking collectives: 27.1 us -> 12 us  [copy_for_each(): return lax.all_to_all(copies, axis, split_axis=0, concat_axis=0, tiled=True)]
  transfers between devices with their start and end apart: 3 -> 7, of which waited for: 3 -> 7; matrix products, arithmetic and copies ran while one was open for 1% -> 1% of each run, Pallas kernels for 0% -> 0%
where the time goes in v1:
time: 327 us; the launch traced here: 326 us
  waiting for transfers between devices  201 us (61%)
  blocking collectives  40.5 us (12%)
  starting transfers between devices  36.6 us (11%)
  matrix products  17.9 us (5%)
  between operations  14.9 us (5%)
  local copies, waits for them, and re-layouts  8.05 us (2%)
  other arithmetic  7.98 us (2%)
    reduce_scatter x1, waiting for transfers between devices, per_device(): lax.psum_scatter(lax.dot_general(grad_pre, cand_rows, (((0,), (0,)), ((),...  101 us
    ppermute x4, waiting for transfers between devices, per_device(): lax.ppermute(summed, 'grp', [(dev, dev ^ hop) for dev in range(16)])  52.2 us
    all_gather x1, waiting for transfers between devices, per_device(): lax.all_gather(hidden_weight, 'cand', axis=0, tiled=True)  38.8 us
    ppermute x4, starting transfers between devices, per_device(): lax.ppermute(summed, 'grp', [(dev, dev ^ hop) for dev in range(16)])  31.2 us
    all_gather x1, blocking collectives, turned_gather(): result = lax.all_gather(both, axis, axis=0, tiled=True)  28.5 us
    all_to_all x1, blocking collectives, copy_for_each(): return lax.all_to_all(copies, axis, split_axis=0, concat_axis=0, tiled=True)  12 us
    dot_general x1, matrix products, per_device(): lax.dot_general(grad_pre, cand_rows, (((0,), (0,)), ((), ())), preferred_...  10.4 us
    all_to_all x1, waiting for transfers between devices, copy_for_each(): return lax.all_to_all(copies, axis, split_axis=0, concat_axis=0, tiled=True)  7.27 us
  transfers between devices with their start and end apart: 7, of which 7 were waited for; matrix products, arithmetic and copies ran while one was open for 1% of the time, Pallas kernels for 0%

profile of v1, /device:TPU:1, one launch (start us, length us, event | category | flops | bytes accessed | tf_op | source)
XLA Modules:
  0.0 326.5 jit_solution(2660351963352656586)
XLA Ops:
  7.2 0.0 copy-start
  7.2 0.0 all-gather.2.cloned.1.call-start
  7.2 0.7 all-gather.2.cloned.1.call-update
  7.9 0.7 reshape.20
  8.6 0.8 copy.28
  9.4 0.8 copy.29
  10.2 0.1 pad_add_fusion
  10.2 28.5 %all_gather.6 = s32[1024,48]{1,0:T(8,128)S(1)} all-gather(s32[32,48]{1,0:T(8,128)S(1)} %pad_add_fusion), channel_id=1, replica_groups=mesh['grp'=16,'cand'=32] {'cand'}, dimensions={0}, use_global_device_ids=true | all-gather | bytes 202752 | tf_op jit(solution)/shard_map/all_gather | solution.py:13
  38.7 0.2 fusion.33
  38.9 0.2 copy.35
  39.1 0.2 copy.36
  39.3 0.1 divide_bitcast_fusion
  39.3 38.8 %all-gather.2.cloned.1.call-done = bf16[2048,1024]{1,0:T(8,128)(2,1)} async-done(((bf16[64,1024]{1,0:T(8,128)(2,1)}), bf16[2048,1024]{1,0:T(8,128)(2,1)}) %all-gather.2.cloned.1.call-update) | async-done | bytes 4194320 | tf_op jit(solution)/shard_map/all_gather | solution.py:71
  78.2 0.0 copy-done
  78.2 5.3 %fusion.34 = f32[768,2048]{1,0:T(8,128)S(1)} fusion(bf16[768,1024]{1,0:T(8,128)(2,1)S(1)} %bitcast.12, bf16[2048,1024]{1,0:T(8,128)(2,1)} %all-gather.2.cloned.1.call-done), kind=kOutput, calls=%fused_computation.49 | convolution fusion | flops 3221225472 | bytes 12058624 | tf_op jit(solution)/shard_map/dot_general | solution.py:69
  83.5 0.0 copy-start.6
  83.5 2.6 copy-done.6
  86.1 0.0 copy-start.1
  86.1 0.0 copy-start.2
  86.1 0.0 copy-start.3
  86.1 0.0 copy-start.5
  86.1 2.2 fusion.22
  88.3 0.1 sub.63
  88.5 0.8 reshape.24
  89.3 5.3 %all-to-all-start = ((f32[32,1,768]{2,1,0:T(1,128)}), f32[32,1,768]{2,1,0:T(1,128)S(1)}, u32[]{:S(2)}, u32[]{:S(2)}) async-start(f32[32,1,768]{2,1,0:T(1,128)} %reshape.24), calls=%async_computation | async-start | bytes 196608 | tf_op jit(solution)/shard_map/all_to_all | solution.py:25
  94.6 0.0 reduce-scatter.2.cloned.1.call-start
  94.7 0.0 copy-done.1
  94.7 0.0 copy-done.2
  94.7 0.0 copy-done.3
  94.7 7.3 %all-to-all-done = f32[32,1,768]{2,1,0:T(1,128)S(1)} async-done(((f32[32,1,768]{2,1,0:T(1,128)}), f32[32,1,768]{2,1,0:T(1,128)S(1)}, u32[]{:S(2)}, u32[]{:S(2)}) %all-to-all-start) | async-done | bytes 98336 | tf_op jit(solution)/shard_map/all_to_all | solution.py:25
  102.0 0.5 broadcast.84
  102.5 0.9 reduce.3
  103.4 0.1 reshape.25
  103.5 0.1 copy.32
  103.6 0.2 sub.65
  103.8 0.0 copy-done.5
  103.8 3.0 fusion.13
  106.8 0.0 copy-start.4
  106.8 0.1 mul.88
  106.9 10.4 %convolution_convert_fusion = bf16[2048,1024]{1,0:T(8,128)(2,1)} fusion(bf16[768,1024]{1,0:T(8,128)(2,1)S(1)} %bitcast.13, f32[768,2048]{1,0:T(8,128)} %copy-done.6, f32[2048]{0:T(1024)S(1)} %convert_element_type.34, f32[768]{0:T(1024)S(1)} %mul.88), kind=kOutput, calls=%fused_computation.19 | convolution fusion | flops 3256352768 | bytes 12069888 | tf_op jit(solution)/shard_map/dot_general | solution.py:95
  117.3 0.0 copy-done.4
  117.3 0.0 reduce-scatter.2.cloned.1.call-update
  117.3 101.5 %reduce-scatter.2.cloned.1.call-done = bf16[64,1024]{1,0:T(8,128)(2,1)} async-done(((bf16[2048,1024]{1,0:T(8,128)(2,1)}), bf16[64,1024]{1,0:T(8,128)(2,1)}) %reduce-scatter.2.cloned.1.call-update) | async-done | bytes 131088 | tf_op jit(solution)/shard_map/reduce_scatter | solution.py:94
  218.8 0.9 convert_element_type.37
  219.7 3.2 collective-permute-start
  222.9 3.9 %collective-permute-done = f32[64,1024]{1,0:T(8,128)S(1)} collective-permute-done((f32[64,1024]{1,0:T(8,128)S(1)}, f32[64,1024]{1,0:T(8,128)S(1)}, u32[]{:S(2)}, u32[]{:S(2)}) %collective-permute-start) | collective-permute-done | bytes 262176 | tf_op jit(solution)/shard_map/ppermute | solution.py:104
  226.8 0.9 convert_add_fusion
  227.8 4.2 %collective-permute-start.1 = (f32[64,1024]{1,0:T(8,128)S(1)}, f32[64,1024]{1,0:T(8,128)S(1)}, u32[]{:S(2)}, u32[]{:S(2)}) collective-permute-start(f32[64,1024]{1,0:T(8,128)S(1)} %convert_add_fusion), channel_id=1, source_target_pairs={{0,64},{32,96},{64,0},{96,32},{128,192},{160,224},{192,128},{224,1... | collective-permute-start | bytes 786440 | tf_op jit(solution)/shard_map/ppermute | solution.py:104
  231.9 11.4 %collective-permute-done.1 = f32[64,1024]{1,0:T(8,128)S(1)} collective-permute-done((f32[64,1024]{1,0:T(8,128)S(1)}, f32[64,1024]{1,0:T(8,128)S(1)}, u32[]{:S(2)}, u32[]{:S(2)}) %collective-permute-start.1) | collective-permute-done | bytes 262176 | tf_op jit(solution)/shard_map/ppermute | solution.py:104
  243.4 7.4 %collective-permute-start.2 = (f32[64,1024]{1,0:T(8,128)S(1)}, f32[64,1024]{1,0:T(8,128)S(1)}, u32[]{:S(2)}, u32[]{:S(2)}) collective-permute-start(f32[64,1024]{1,0:T(8,128)S(1)} %add.51), channel_id=1, source_target_pairs={{0,128},{32,160},{64,192},{96,224},{128,0},{160,32},{192,64},{224,... | collective-permute-start | bytes 786440 | tf_op jit(solution)/shard_map/ppermute | solution.py:104
  250.7 22.6 %collective-permute-done.2 = f32[64,1024]{1,0:T(8,128)S(1)} collective-permute-done((f32[64,1024]{1,0:T(8,128)S(1)}, f32[64,1024]{1,0:T(8,128)S(1)}, u32[]{:S(2)}, u32[]{:S(2)}) %collective-permute-start.2) | collective-permute-done | bytes 262176 | tf_op jit(solution)/shard_map/ppermute | solution.py:104
  273.4 16.5 %collective-permute-start.3 = (f32[64,1024]{1,0:T(8,128)S(1)}, f32[64,1024]{1,0:T(8,128)S(1)}, u32[]{:S(2)}, u32[]{:S(2)}) collective-permute-start(f32[64,1024]{1,0:T(8,128)S(1)} %add.52), channel_id=1, source_target_pairs={{0,256},{32,288},{64,320},{96,352},{128,384},{160,416},{192,448},{... | collective-permute-start | bytes 786440 | tf_op jit(solution)/shard_map/ppermute | solution.py:104
  289.9 14.3 %collective-permute-done.3 = f32[64,1024]{1,0:T(8,128)S(1)} collective-permute-done((f32[64,1024]{1,0:T(8,128)S(1)}, f32[64,1024]{1,0:T(8,128)S(1)}, u32[]{:S(2)}, u32[]{:S(2)}) %collective-permute-start.3) | collective-permute-done | bytes 262176 | tf_op jit(solution)/shard_map/ppermute | solution.py:104
  304.2 0.7 multiply_reduce_fusion
  304.9 0.7 broadcast_in_dim.5
  305.6 12.0 %all_to_all.11 = f32[32,1,1]{2,1,0:T(1,128)S(1)} all-to-all(f32[32,1,1]{2,1,0:T(1,128)S(1)} %broadcast_in_dim.5), channel_id=1, replica_groups=mesh['grp'=16,'cand'=32] {'cand'}, dimensions={0} | all-to-all | bytes 256 | tf_op jit(solution)/shard_map/all_to_all | solution.py:25
  317.6 0.6 reduce_sum.29
  318.9 0.7 broadcast_multiply_fusion
  (5 shorter events, 0.1 us)
Async XLA Ops:
  7.2 71.0 %copy-start = (bf16[24,32,1024]{2,1,0:T(8,128)(2,1)S(1)}, bf16[24,32,1024]{2,1,0:T(8,128)(2,1)}, u32[]{:S(2)}) copy-start(bf16[24,32,1024]{2,1,0:T(8,128)(2,1)} %param.6) | copy-start | bytes 4718596
  7.2 71.0 %all-gather.2.cloned.1.call-start = ((), (), s32[]{:S(2)}) async-start(), calls=%async_computation.3 | async-start | bytes 4325376 | tf_op jit(solution)/shard_map/all_gather | solution.py:71
  83.5 2.6 copy-start.6
  86.1 8.6 %copy-start.1 = (s32[24,32]{1,0:T(8,128)S(1)}, s32[24,32]{1,0:T(8,128)}, u32[]{:S(2)}) copy-start(s32[24,32]{1,0:T(8,128)} %param.10) | copy-start | bytes 9220
  86.1 8.6 %copy-start.2 = (s32[24,32]{1,0:T(8,128)S(1)}, s32[24,32]{1,0:T(8,128)}, u32[]{:S(2)}) copy-start(s32[24,32]{1,0:T(8,128)} %param.9) | copy-start | bytes 9220
  86.1 8.6 %copy-start.3 = (bf16[2048]{0:T(1024)(128)(2,1)S(1)}, bf16[2048]{0:T(1024)(128)(2,1)}, u32[]{:S(2)}) copy-start(bf16[2048]{0:T(1024)(128)(2,1)} %param.8) | copy-start | bytes 12292
  86.1 17.7 %copy-start.5 = (f32[24]{0:T(128)S(1)}, f32[24]{0:T(128)}, u32[]{:S(2)}) copy-start(f32[24]{0:T(128)} %param.11) | copy-start | bytes 292
  89.3 12.7 %all-to-all-start = ((f32[32,1,768]{2,1,0:T(1,128)}), f32[32,1,768]{2,1,0:T(1,128)S(1)}, u32[]{:S(2)}, u32[]{:S(2)}) async-start(f32[32,1,768]{2,1,0:T(1,128)} %reshape.24), calls=%async_computation | async-start | bytes 196608 | tf_op jit(solution)/shard_map/all_to_all | solution.py:25
  94.6 124.2 %reduce-scatter.2.cloned.1.call-start = ((), (), s32[]{:S(2)}) async-start(), calls=%async_computation.4 | async-start | bytes 4325376 | tf_op jit(solution)/shard_map/reduce_scatter | solution.py:94
  106.8 10.5 %copy-start.4 = (f32[24,32]{1,0:T(8,128)}, f32[24,32]{1,0:T(8,128)S(1)}, u32[]{:S(2)}) copy-start(f32[24,32]{1,0:T(8,128)S(1)} %fusion.13) | copy-start | bytes 9220
  219.7 7.1 %collective-permute-start = (f32[64,1024]{1,0:T(8,128)S(1)}, f32[64,1024]{1,0:T(8,128)S(1)}, u32[]{:S(2)}, u32[]{:S(2)}) collective-permute-start(f32[64,1024]{1,0:T(8,128)S(1)} %convert_element_type.37), channel_id=1, source_target_pairs={{0,32},{32,0},{64,96},{96,64},{128,160},{160,128},{192,224},{224,1... | collective-permute-start | bytes 786440 | tf_op jit(solution)/shard_map/ppermute | solution.py:104
  227.8 15.6 %collective-permute-start.1 = (f32[64,1024]{1,0:T(8,128)S(1)}, f32[64,1024]{1,0:T(8,128)S(1)}, u32[]{:S(2)}, u32[]{:S(2)}) collective-permute-start(f32[64,1024]{1,0:T(8,128)S(1)} %convert_add_fusion), channel_id=1, source_target_pairs={{0,64},{32,96},{64,0},{96,32},{128,192},{160,224},{192,128},{224,1... | collective-permute-start | bytes 786440 | tf_op jit(solution)/shard_map/ppermute | solution.py:104
  243.4 30.0 %collective-permute-start.2 = (f32[64,1024]{1,0:T(8,128)S(1)}, f32[64,1024]{1,0:T(8,128)S(1)}, u32[]{:S(2)}, u32[]{:S(2)}) collective-permute-start(f32[64,1024]{1,0:T(8,128)S(1)} %add.51), channel_id=1, source_target_pairs={{0,128},{32,160},{64,192},{96,224},{128,0},{160,32},{192,64},{224,... | collective-permute-start | bytes 786440 | tf_op jit(solution)/shard_map/ppermute | solution.py:104
  273.4 30.9 %collective-permute-start.3 = (f32[64,1024]{1,0:T(8,128)S(1)}, f32[64,1024]{1,0:T(8,128)S(1)}, u32[]{:S(2)}, u32[]{:S(2)}) collective-permute-start(f32[64,1024]{1,0:T(8,128)S(1)} %add.52), channel_id=1, source_target_pairs={{0,256},{32,288},{64,320},{96,352},{128,384},{160,416},{192,448},{... | collective-permute-start | bytes 786440 | tf_op jit(solution)/shard_map/ppermute | solution.py:104
Sparse Core Ops, SparseCore 0:
  11.1 67.0 all-gather.1
  117.4 101.2 reduce-scatter.1
